TPU v7x, 32 devices: a whole 2x2x4 slice. The times are simulated.
32 devices in a mesh: pair: 8 (over z, x), sector: 4 (over y, core).
Axes of the slice: x: 2, y: 2, z: 4, core: 2. Of those that a mesh axis runs over, the one named last changes fastest.
Arguments:
- wave: bfloat16 [4, 1024, 1024], P('sector', 'pair'), may hold values from -6 to 6
- left_ops: bfloat16 [16, 4, 1024, 1024], P('pair', 'sector'), may hold values from -0.1875 to 0.1875
- right_ops: bfloat16 [16, 4, 1024, 1024], P('pair', 'sector'), may hold values from -0.046875 to 0.046875
- targets: int32 [16, 4], P('pair', 'sector'), may hold values from -1 to 3
- sector_sizes: int32 [4], replicated, may hold values from 256 to 1024
- pair_ids: int32 [16], P('pair'), may hold values from 0 to 15, each once
- pair_coefficients: float32 [16], replicated, may hold values from 0.25 to 2
Outputs:
- sigma_blocks: float32 [4, 1024, 1024], P('sector', 'pair')
Inputs may be any that keep to these rules, and one draw needn't show every extreme that they name: `pair_ids`: each orbital pair once.
All inputs are finite; a program needn't handle non-finite values.
Results may differ from a plain program's by a relative error of at most 0.0029.
Values may be sent and summed in bfloat16 or wider, within the bound.
No kernel may reach another device: no remote copies, remote signals or barrier semaphores. Data moves between devices by JAX's collectives and lax.ppermute only.
A program may use at most 128 MiB of HBM per device.

v0:
```python
import jax
import jax.numpy as jnp
from jax import lax
from jax.sharding import PartitionSpec as P


def body(wave, left_ops, right_ops, targets, sector_sizes, pair_ids, pair_coefficients):
    block = wave.shape[2]
    local_rows = wave.shape[1]
    pair_slots = left_ops.shape[0]
    sectors = sector_sizes.shape[0]
    pair_count = lax.axis_size("pair")
    own_sector = lax.axis_index("sector")
    sector_ids = jnp.arange(sectors, dtype=jnp.int32)
    own_size = jnp.sum(jnp.where(sector_ids == own_sector, sector_sizes, 0))
    col_ids = jnp.arange(block, dtype=jnp.int32)
    row_ids = lax.axis_index("pair") * local_rows + jnp.arange(local_rows, dtype=jnp.int32)
    col_used = col_ids < own_size
    row_used = row_ids < own_size
    masked = wave[0] * (row_used[:, None] & col_used[None, :]).astype(wave.dtype)
    table_ids = jnp.arange(pair_coefficients.shape[0], dtype=jnp.int32)
    factor = jnp.sum(
        jnp.where(pair_ids[:, None] == table_ids[None, :], pair_coefficients[None, :], 0.0), axis=1
    )
    left_mats = left_ops[:, 0]
    right_mats = right_ops[:, 0]
    chosen_targets = targets[:, 0]
    totals = jnp.zeros((sectors, block, block), jnp.float32)
    gathered = lax.all_gather(masked, "pair", axis=0, tiled=True)
    for member in range(pair_slots):
        target = chosen_targets[member]
        left_mat = left_mats[member]
        right_mat = right_mats[member]
        weight = factor[member]

        def present_term(left_mat=left_mat, right_mat=right_mat, weight=weight):
            left = jnp.dot(left_mat, gathered, preferred_element_type=jnp.float32).astype(
                jnp.bfloat16
            )
            term = lax.dot_general(
                left, right_mat, (((1,), (1,)), ((), ())), preferred_element_type=jnp.float32
            )
            return weight * term

        def absent_term():
            return jnp.zeros((block, block), jnp.float32)

        addition = lax.cond(target >= 0, present_term, absent_term)
        place = jnp.maximum(target, 0)
        current = lax.dynamic_index_in_dim(totals, place, 0, keepdims=False)
        totals = lax.dynamic_update_index_in_dim(totals, current + addition, place, 0)
    arranged = totals.reshape(sectors, pair_count, local_rows, block).transpose(1, 0, 2, 3)
    arranged = arranged.reshape(pair_count * sectors * local_rows, block)
    summed = lax.psum_scatter(arranged, ("pair", "sector"), scatter_dimension=0, tiled=True)[None]
    out_mask = (row_used[:, None] & col_used[None, :]).astype(jnp.float32)
    return summed * out_mask[None]


def solution(mesh):
    placed = (
        P("sector", "pair", None),
        P("pair", "sector", None, None),
        P("pair", "sector", None, None),
        P("pair", "sector"),
        P(),
        P("pair"),
        P(),
    )
    return jax.shard_map(
        body, mesh=mesh, in_specs=placed, out_specs=P("sector", "pair", None), check_vma=False
    )
```

profile of v0, /device:TPU:3, one launch (start us, length us, event | category | flops | bytes accessed | tf_op | source)
XLA Modules:
  0.0 304.2 jit_solution(10852317030803112737)
XLA Ops:
  6.5 1.3 fusion.22
  7.8 0.6 iota_compare_fusion
  8.5 0.7 add_compare_fusion
  9.1 1.8 and_select_fusion.1
  11.0 0.0 all-gather.2.cloned.1.call-update
  11.0 0.0 reduce-scatter.2.cloned.1.call-start
  11.0 1.3 fusion.23
  14.8 0.9 fusion.21
  15.7 43.0 %all-gather.2.cloned.1.call-done = bf16[1024,1024]{1,0:T(8,128)(2,1)} async-done(((bf16[128,1024]{1,0:T(8,128)(2,1)}), bf16[1024,1024]{1,0:T(8,128)(2,1)}) %all-gather.2.cloned.1.call-update) | async-done | bytes 2097168 | tf_op jit(solution)/shard_map/all_gather | solution.py:29
  58.6 2.5 conditional.2
  58.6 2.5 broadcast_in_dim.32
  61.1 2.1 broadcast_in_dim.40
  63.3 0.0 copy-done.1
  63.3 0.6 constant_dynamic-update-slice_fusion
  63.9 5.7 %copy-done = f32[4,1024,1024]{2,1,0:T(8,128)} copy-done((f32[4,1024,1024]{2,1,0:T(8,128)}, f32[4,1024,1024]{2,1,0:T(8,128)S(1)}, u32[]{:S(2)}) %copy-start) | copy-done | bytes 16777240
  69.7 2.2 constant_dynamic-slice_fusion
  71.9 10.6 %conditional.3 = (f32[1024,1024]{1,0:T(8,128)}) conditional(s32[]{:T(128)} %bitcast.12, () %tuple.21, (f32[2]{0:T(128)S(1)}, bf16[2,1,1024,1024]{3,2,1,0:T(8,128)(2,1)}, bf16[1024,1024]{1,0:T(8,128)(2,1)}, bf16[2,1,1024,1024]{3,2,1,0:T(8,128)(2,1)}) %tuple.20), branch_computations={%region_4.5_spmd, %region_5.6_spmd} | conditional | flops 4297064448 | bytes 10486288 | solution.py:48
  71.9 0.6 slice.31
  72.5 10.0 %convolution_multiply_fusion = f32[1024,1024]{1,0:T(8,128)} fusion(bf16[2,1,1024,1024]{3,2,1,0:T(8,128)(2,1)} %get-tuple-element.47, f32[]{:T(128)} %bitcast.4, bf16[1024,1024]{1,0:T(8,128)(2,1)} %get-tuple-element.46, bf16[2,1,1024,1024]{3,2,1,0:T(8,128)(2,1)} %get-tuple-element.45), kind=kOutput, calls=%fused_computation.7 | convolution fusion | flops 4297064448 | bytes 10486272 | tf_op jit(solution)/shard_map/cond/branch_1_fun/dot_general | solution.py:40
  82.5 6.8 %bitcast_dynamic-update-slice_fusion = f32[4,1024,1024]{2,1,0:T(8,128)} fusion(f32[4,1024,1024]{2,1,0:T(8,128)} %copy-done, s32[]{:T(128)} %bitcast.10, f32[1024,1024]{1,0:T(8,128)} %get-tuple-element.51, f32[1,1024,1024]{2,1,0:T(8,128)} %constant_dynamic-slice_fusion), kind=kLoop, calls=%fused_computation.14 | loop fusion | flops 1048576 | bytes 12583424 | tf_op jit(solution)/shard_map/jit(dynamic_update_index_in_dim)/dynamic_update_slice | solution.py:51
  89.2 11.8 %copy.9 = f32[8,4,128,1024]{3,2,1,0:T(8,128)} copy(f32[8,4,128,1024]{3,2,0,1:T(8,128)} %bitcast.45) | data formatting | bytes 33554432 | tf_op jit(solution)/shard_map/transpose | solution.py:52
  101.0 0.0 reduce-scatter.2.cloned.1.call-update
  101.1 194.3 %reduce-scatter.2.cloned.1.call-done = f32[128,1024]{1,0:T(8,128)} async-done(((f32[4096,1024]{1,0:T(8,128)}), f32[128,1024]{1,0:T(8,128)}) %reduce-scatter.2.cloned.1.call-update) | async-done | bytes 524304 | tf_op jit(solution)/shard_map/reduce_scatter | solution.py:54
  295.4 2.0 fusion.20
  (3 shorter events, 0.0 us)
Async XLA Ops:
  6.5 52.1 %all-gather.2.cloned.1.call-start = ((), (), s32[]{:S(2)}) async-start(), calls=%async_computation.1 | async-start | bytes 2359296 | tf_op jit(solution)/shard_map/all_gather | solution.py:29
  11.0 284.4 %reduce-scatter.2.cloned.1.call-start = ((), (), s32[]{:S(2)}) async-start(), calls=%async_computation.2 | async-start | bytes 17301504 | tf_op jit(solution)/shard_map/reduce_scatter | solution.py:54
  61.1 2.2 copy-start.1
  63.9 5.7 %copy-start = (f32[4,1024,1024]{2,1,0:T(8,128)}, f32[4,1024,1024]{2,1,0:T(8,128)S(1)}, u32[]{:S(2)}) copy-start(f32[4,1024,1024]{2,1,0:T(8,128)S(1)} %constant_dynamic-update-slice_fusion) | copy-start | bytes 50331652
Sparse Core Ops, SparseCore 0:
  11.1 47.4 all-gather.1
  101.2 194.1 reduce-scatter.1
where the time goes:
time: 305 us; the launch traced here: 304 us
  waiting for transfers between devices  237 us (78%)
  local copies, waits for them, and re-layouts  27 us (9%)
  between operations  15.9 us (5%)
  other arithmetic  14 us (5%)
  matrix products  9.97 us (3%)
    reduce_scatter x1, waiting for transfers between devices, body(): lax.psum_scatter(arranged, ('pair', 'sector'), scatter_dimension=0, tiled...  194 us
    all_gather x1, waiting for transfers between devices, body(): gathered = lax.all_gather(masked, 'pair', axis=0, tiled=True)  43 us
    transpose x1, local copies, waits for them, and re-layouts, body(): totals.reshape(sectors, pair_count, local_rows, block).transpose(1, 0, 2, 3)  11.8 us
    dot_general x1, matrix products, present_term(): lax.dot_general(left, right_mat, (((1,), (1,)), ((), ())), preferred_elem...  9.97 us
    dynamic_update_slice x1, other arithmetic, body(): lax.dynamic_update_index_in_dim(totals, current + addition, place, 0)  6.78 us
  transfers between devices with their start and end apart: 2, of which 2 were waited for; matrix products, arithmetic and copies ran while one was open for 1% of the time, Pallas kernels for 0%

commit v1 on v0

--- a/solution.py
+++ b/solution.py
@@ -2,6 +2,17 @@
 import jax.numpy as jnp
 from jax import lax
 from jax.sharding import PartitionSpec as P
+
+
+def around_the_ring(block, axis, dim):
+    size = lax.axis_size(axis)
+    right = [(i, (i + 1) % size) for i in range(size)]
+    terms = [block]
+    for reach in range(1, size):
+        terms = [lax.ppermute(terms[0], axis, right), *terms]
+    whole = jnp.concatenate(terms, axis=dim)
+    offset = (lax.axis_index(axis) + 1) * terms[-1].shape[dim]
+    return jnp.roll(whole, offset, axis=dim)
 
 
 def body(wave, left_ops, right_ops, targets, sector_sizes, pair_ids, pair_coefficients):
@@ -26,7 +37,7 @@
     right_mats = right_ops[:, 0]
     chosen_targets = targets[:, 0]
     totals = jnp.zeros((sectors, block, block), jnp.float32)
-    gathered = lax.all_gather(masked, "pair", axis=0, tiled=True)
+    gathered = around_the_ring(masked, "pair", 0)
     for member in range(pair_slots):
         target = chosen_targets[member]
         left_mat = left_mats[member]

time: 305 us -> 321 us (1.052)
  waiting for transfers between devices: 237 us -> 248 us
  starting transfers between devices: 0.04 us -> 4.14 us
    ppermute x0 -> x7, waiting for transfers between devices: none -> 47.2 us  [around_the_ring(): terms = [lax.ppermute(terms[0], axis, right), *terms]]
    all_gather x1 -> x0, waiting for transfers between devices: 43 us -> none  [body(): gathered = lax.all_gather(masked, 'pair', axis=0, tiled=True)]
    reduce_scatter x1, waiting for transfers between devices: 194 us -> 200 us  [body(): lax.psum_scatter(arranged, ('pair', 'sector'), scatter_dimension=0, tiled...]
    ppermute x0 -> x7, starting transfers between devices: none -> 4.14 us  [around_the_ring(): terms = [lax.ppermute(terms[0], axis, right), *terms]]
  transfers between devices with their start and end apart: 2 -> 8, of which waited for: 2 -> 8; matrix products, arithmetic and copies ran while one was open for 1% -> 1% of each run, Pallas kernels for 0% -> 0%
where the time goes in v1:
time: 321 us; the launch traced here: 320 us
  waiting for transfers between devices  248 us (77%)
  local copies, waits for them, and re-layouts  28.8 us (9%)
  between operations  16.3 us (5%)
  other arithmetic  13.6 us (4%)
  matrix products  9.98 us (3%)
  starting transfers between devices  4.14 us (1%)
    reduce_scatter x1, waiting for transfers between devices, body(): lax.psum_scatter(arranged, ('pair', 'sector'), scatter_dimension=0, tiled...  200 us
    ppermute x7, waiting for transfers between devices, around_the_ring(): terms = [lax.ppermute(terms[0], axis, right), *terms]  47.2 us
    transpose x1, local copies, waits for them, and re-layouts, body(): totals.reshape(sectors, pair_count, local_rows, block).transpose(1, 0, 2, 3)  11.8 us
    dot_general x1, matrix products, present_term(): lax.dot_general(left, right_mat, (((1,), (1,)), ((), ())), preferred_elem...  9.98 us
    dynamic_update_slice x1, other arithmetic, body(): lax.dynamic_update_index_in_dim(totals, current + addition, place, 0)  6.79 us
  transfers between devices with their start and end apart: 8, of which 8 were waited for; matrix products, arithmetic and copies ran while one was open for 1% of the time, Pallas kernels for 0%

profile of v1, /device:TPU:3, one launch (start us, length us, event | category | flops | bytes accessed | tf_op | source)
XLA Modules:
  0.0 320.3 jit_solution(11338605324247451129)
XLA Ops:
  6.5 1.3 fusion.22
  9.2 1.1 and_select_fusion.1
  10.3 1.3 collective-permute-start
  11.6 5.9 %collective-permute-done = bf16[128,1024]{1,0:T(8,128)(2,1)S(1)} collective-permute-done((bf16[128,1024]{1,0:T(8,128)(2,1)S(1)}, bf16[128,1024]{1,0:T(8,128)(2,1)S(1)}, u32[]{:S(2)}, u32[]{:S(2)}) %collective-permute-start) | collective-permute-done | bytes 262176 | tf_op jit(solution)/shard_map/ppermute | solution.py:12
  17.5 2.2 collective-permute-start.1
  19.7 6.6 %collective-permute-done.1 = bf16[128,1024]{1,0:T(8,128)(2,1)S(1)} collective-permute-done((bf16[128,1024]{1,0:T(8,128)(2,1)S(1)}, bf16[128,1024]{1,0:T(8,128)(2,1)S(1)}, u32[]{:S(2)}, u32[]{:S(2)}) %collective-permute-start.1) | collective-permute-done | bytes 262176 | tf_op jit(solution)/shard_map/ppermute | solution.py:12
  26.9 7.8 %collective-permute-done.2 = bf16[128,1024]{1,0:T(8,128)(2,1)S(1)} collective-permute-done((bf16[128,1024]{1,0:T(8,128)(2,1)S(1)}, bf16[128,1024]{1,0:T(8,128)(2,1)S(1)}, u32[]{:S(2)}, u32[]{:S(2)}) %collective-permute-start.2) | collective-permute-done | bytes 262176 | tf_op jit(solution)/shard_map/ppermute | solution.py:12
  34.8 7.6 %collective-permute-done.3 = bf16[128,1024]{1,0:T(8,128)(2,1)S(1)} collective-permute-done((bf16[128,1024]{1,0:T(8,128)(2,1)S(1)}, bf16[128,1024]{1,0:T(8,128)(2,1)S(1)}, u32[]{:S(2)}, u32[]{:S(2)}) %collective-permute-start.3) | collective-permute-done | bytes 262176 | tf_op jit(solution)/shard_map/ppermute | solution.py:12
  42.4 7.9 %collective-permute-done.4 = bf16[128,1024]{1,0:T(8,128)(2,1)S(1)} collective-permute-done((bf16[128,1024]{1,0:T(8,128)(2,1)S(1)}, bf16[128,1024]{1,0:T(8,128)(2,1)S(1)}, u32[]{:S(2)}, u32[]{:S(2)}) %collective-permute-start.4) | collective-permute-done | bytes 262176 | tf_op jit(solution)/shard_map/ppermute | solution.py:12
  50.3 7.9 %collective-permute-done.5 = bf16[128,1024]{1,0:T(8,128)(2,1)S(1)} collective-permute-done((bf16[128,1024]{1,0:T(8,128)(2,1)S(1)}, bf16[128,1024]{1,0:T(8,128)(2,1)S(1)}, u32[]{:S(2)}, u32[]{:S(2)}) %collective-permute-start.5) | collective-permute-done | bytes 262176 | tf_op jit(solution)/shard_map/ppermute | solution.py:12
  58.2 1.3 fusion.23
  63.1 3.4 %collective-permute-done.6 = bf16[128,1024]{1,0:T(8,128)(2,1)S(1)} collective-permute-done((bf16[128,1024]{1,0:T(8,128)(2,1)S(1)}, bf16[128,1024]{1,0:T(8,128)(2,1)S(1)}, u32[]{:S(2)}, u32[]{:S(2)}) %collective-permute-start.6) | collective-permute-done | bytes 262176 | tf_op jit(solution)/shard_map/ppermute | solution.py:12
  67.2 1.5 constant_dynamic-slice_fusion.1
  68.7 2.5 conditional.2
  68.7 2.5 broadcast_in_dim.32
  71.2 2.1 broadcast_in_dim.40
  74.0 5.7 %copy-done = f32[4,1024,1024]{2,1,0:T(8,128)} copy-done((f32[4,1024,1024]{2,1,0:T(8,128)}, f32[4,1024,1024]{2,1,0:T(8,128)S(1)}, u32[]{:S(2)}) %copy-start) | copy-done | bytes 16777240
  79.8 2.2 constant_dynamic-slice_fusion
  82.0 10.6 %conditional.3 = (f32[1024,1024]{1,0:T(8,128)}) conditional(s32[]{:T(128)} %bitcast.12, () %tuple.21, (f32[2]{0:T(128)S(1)}, bf16[2,1,1024,1024]{3,2,1,0:T(8,128)(2,1)}, bf16[1024,1024]{1,0:T(8,128)(2,1)}, bf16[2,1,1024,1024]{3,2,1,0:T(8,128)(2,1)}) %tuple.20), branch_computations={%region_4.5_spmd, %region_5.6_spmd} | conditional | flops 4297064448 | bytes 10486288 | solution.py:59
  82.6 10.0 %convolution_multiply_fusion = f32[1024,1024]{1,0:T(8,128)} fusion(bf16[2,1,1024,1024]{3,2,1,0:T(8,128)(2,1)} %get-tuple-element.47, f32[]{:T(128)} %bitcast.4, bf16[1024,1024]{1,0:T(8,128)(2,1)} %get-tuple-element.46, bf16[2,1,1024,1024]{3,2,1,0:T(8,128)(2,1)} %get-tuple-element.45), kind=kOutput, calls=%fused_computation.7 | convolution fusion | flops 4297064448 | bytes 10486272 | tf_op jit(solution)/shard_map/cond/branch_1_fun/dot_general | solution.py:51
  92.6 6.8 %bitcast_dynamic-update-slice_fusion = f32[4,1024,1024]{2,1,0:T(8,128)} fusion(f32[4,1024,1024]{2,1,0:T(8,128)} %copy-done, s32[]{:T(128)} %bitcast.10, f32[1024,1024]{1,0:T(8,128)} %get-tuple-element.51, f32[1,1024,1024]{2,1,0:T(8,128)} %constant_dynamic-slice_fusion), kind=kLoop, calls=%fused_computation.14 | loop fusion | flops 1048576 | bytes 12583424 | tf_op jit(solution)/shard_map/jit(dynamic_update_index_in_dim)/dynamic_update_slice | solution.py:62
  99.4 11.8 %copy.9 = f32[8,4,128,1024]{3,2,1,0:T(8,128)} copy(f32[8,4,128,1024]{3,2,0,1:T(8,128)} %bitcast.49) | data formatting | bytes 33554432 | tf_op jit(solution)/shard_map/transpose | solution.py:63
  111.2 200.4 %reduce-scatter.2.cloned.1.call-done = f32[128,1024]{1,0:T(8,128)} async-done(((f32[4096,1024]{1,0:T(8,128)}), f32[128,1024]{1,0:T(8,128)}) %reduce-scatter.2.cloned.1.call-update) | async-done | bytes 524304 | tf_op jit(solution)/shard_map/reduce_scatter | solution.py:65
  311.5 2.0 fusion.20
  (33 shorter events, 4.7 us)
Async XLA Ops:
  6.5 60.1 %copy-start.2 = (bf16[1,128,1024]{2,1,0:T(8,128)(2,1)S(1)}, bf16[1,128,1024]{2,1,0:T(8,128)(2,1)}, u32[]{:S(2)}) copy-start(bf16[1,128,1024]{2,1,0:T(8,128)(2,1)} %param.11) | copy-start | bytes 786436
  6.5 305.0 %reduce-scatter.2.cloned.1.call-start = ((), (), s32[]{:S(2)}) async-start(), calls=%async_computation.1 | async-start | bytes 17301504 | tf_op jit(solution)/shard_map/reduce_scatter | solution.py:65
  10.3 7.2 %collective-permute-start = (bf16[128,1024]{1,0:T(8,128)(2,1)S(1)}, bf16[128,1024]{1,0:T(8,128)(2,1)S(1)}, u32[]{:S(2)}, u32[]{:S(2)}) collective-permute-start(bf16[128,1024]{1,0:T(8,128)(2,1)S(1)} %and_select_fusion.1), channel_id=1, source_target_pairs={{0,4},{4,8},{8,12},{12,16},{16,20},{20,24},{24,28},{28,0},{1,5},{5... | collective-permute-start | bytes 786440 | tf_op jit(solution)/shard_map/ppermute | solution.py:12
  17.5 8.8 %collective-permute-start.1 = (bf16[128,1024]{1,0:T(8,128)(2,1)S(1)}, bf16[128,1024]{1,0:T(8,128)(2,1)S(1)}, u32[]{:S(2)}, u32[]{:S(2)}) collective-permute-start(bf16[128,1024]{1,0:T(8,128)(2,1)S(1)} %collective-permute-done), channel_id=1, source_target_pairs={{0,4},{4,8},{8,12},{12,16},{16,20},{20,24},{24,28},{28,0},{1,5},{5... | collective-permute-start | bytes 786440 | tf_op jit(solution)/shard_map/ppermute | solution.py:12
  26.3 8.5 %collective-permute-start.2 = (bf16[128,1024]{1,0:T(8,128)(2,1)S(1)}, bf16[128,1024]{1,0:T(8,128)(2,1)S(1)}, u32[]{:S(2)}, u32[]{:S(2)}) collective-permute-start(bf16[128,1024]{1,0:T(8,128)(2,1)S(1)} %collective-permute-done.1), channel_id=1, source_target_pairs={{0,4},{4,8},{8,12},{12,16},{16,20},{20,24},{24,28},{28,0},{1,5},{5... | collective-permute-start | bytes 786440 | tf_op jit(solution)/shard_map/ppermute | solution.py:12
  34.8 7.6 %collective-permute-start.3 = (bf16[128,1024]{1,0:T(8,128)(2,1)S(1)}, bf16[128,1024]{1,0:T(8,128)(2,1)S(1)}, u32[]{:S(2)}, u32[]{:S(2)}) collective-permute-start(bf16[128,1024]{1,0:T(8,128)(2,1)S(1)} %collective-permute-done.2), channel_id=1, source_target_pairs={{0,4},{4,8},{8,12},{12,16},{16,20},{20,24},{24,28},{28,0},{1,5},{5... | collective-permute-start | bytes 786440 | tf_op jit(solution)/shard_map/ppermute | solution.py:12
  42.4 7.9 %collective-permute-start.4 = (bf16[128,1024]{1,0:T(8,128)(2,1)S(1)}, bf16[128,1024]{1,0:T(8,128)(2,1)S(1)}, u32[]{:S(2)}, u32[]{:S(2)}) collective-permute-start(bf16[128,1024]{1,0:T(8,128)(2,1)S(1)} %collective-permute-done.3), channel_id=1, source_target_pairs={{0,4},{4,8},{8,12},{12,16},{16,20},{20,24},{24,28},{28,0},{1,5},{5... | collective-permute-start | bytes 786440 | tf_op jit(solution)/shard_map/ppermute | solution.py:12
  50.3 7.9 %collective-permute-start.5 = (bf16[128,1024]{1,0:T(8,128)(2,1)S(1)}, bf16[128,1024]{1,0:T(8,128)(2,1)S(1)}, u32[]{:S(2)}, u32[]{:S(2)}) collective-permute-start(bf16[128,1024]{1,0:T(8,128)(2,1)S(1)} %collective-permute-done.4), channel_id=1, source_target_pairs={{0,4},{4,8},{8,12},{12,16},{16,20},{20,24},{24,28},{28,0},{1,5},{5... | collective-permute-start | bytes 786440 | tf_op jit(solution)/shard_map/ppermute | solution.py:12
  58.2 8.2 %collective-permute-start.6 = (bf16[128,1024]{1,0:T(8,128)(2,1)S(1)}, bf16[128,1024]{1,0:T(8,128)(2,1)S(1)}, u32[]{:S(2)}, u32[]{:S(2)}) collective-permute-start(bf16[128,1024]{1,0:T(8,128)(2,1)S(1)} %collective-permute-done.5), channel_id=1, source_target_pairs={{0,4},{4,8},{8,12},{12,16},{16,20},{20,24},{24,28},{28,0},{1,5},{5... | collective-permute-start | bytes 786440 | tf_op jit(solution)/shard_map/ppermute | solution.py:12
  71.2 2.2 copy-start.1
  74.0 5.7 %copy-start = (f32[4,1024,1024]{2,1,0:T(8,128)}, f32[4,1024,1024]{2,1,0:T(8,128)S(1)}, u32[]{:S(2)}) copy-start(f32[4,1024,1024]{2,1,0:T(8,128)S(1)} %constant_dynamic-update-slice_fusion.16) | copy-start | bytes 50331652
Sparse Core Ops, SparseCore 0:
  111.3 200.1 reduce-scatter.1
